TPU v7x, 32 devices: a whole 2x2x4 slice. The times are simulated.
32 devices in a mesh: bead: 8 (over z, core), atom: 4 (over y, x).
Axes of the slice: x: 2, y: 2, z: 4, core: 2. Of those that a mesh axis runs over, the one named last changes fastest.
Arguments:
- positions: float32 [32, 3, 4096], P('bead', None, 'atom'), may hold values from -6 to 6
- momenta: float32 [32, 3, 4096], P('bead', None, 'atom'), may hold values from -6 to 6
- charge: float32 [4096], P('atom'), may hold values from -1 to 1
- masses: float32 [4096], P('atom'), may hold values from 0.5 to 4
- pair_local: int32 [128], P('atom'), may hold values from 0 to 31, as said below
- pair_other: int32 [128], P('atom'), may hold values from 0 to 31, as said below
- pair_count: int32 [4], P('atom'), may hold values from 0 to 32, as said below
Outputs:
- new_positions: float32 [32, 3, 4096], P('bead', None, 'atom')
- new_momenta: float32 [32, 3, 4096], P('bead', None, 'atom')
- spring: float32 [4096], P('atom')
Inputs may be any that keep to these rules, and one draw needn't show every extreme that they name: `pair_local`: the slots of atom block d (slots d * 32 to (d + 1) * 32 - 1) name tiles of that block: d * 8 to (d + 1) * 8 - 1. `pair_other`: each slot's neighbour tile lies within 8 tiles of its tile, counting cyclically over 32 tiles. `pair_count`: the counts of blocks d and d + 2 sum to at most 32.
All inputs are finite; a program needn't handle non-finite values.
Results may differ from a plain program's by a relative error of at most 0.000071.
Values sent between devices are 32-bit elements; how exact they have to be, the bound alone decides.
A program may use at most 64 MiB of HBM per device.

v0:
```python
import jax
import jax.numpy as jnp
from jax import lax
from jax.sharding import PartitionSpec as P

time_step = 1.0
omega_cycle = 1.2
width_sq = 2.0


def extended(block, sides, width):
    for axis, dim in sides:
        count = lax.axis_size(axis)
        forward = [(i, i + 1) for i in range(count - 1)]
        forward.append((count - 1, 0))
        backward = [(target, source) for source, target in forward]
        low = lax.ppermute(
            lax.slice_in_dim(block, block.shape[dim] - width, None, axis=dim), axis, forward
        )
        high = lax.ppermute(lax.slice_in_dim(block, 0, width, axis=dim), axis, backward)
        block = jnp.concatenate([low, block, high], axis=dim)
    return block


def cycle_table(beads):
    bead_index = jnp.arange(beads, dtype=jnp.float32)[:, None]
    mode_index = jnp.arange(beads, dtype=jnp.float32)[None, :]
    middle = beads // 2
    angle = 2.0 * jnp.pi * bead_index * mode_index / beads
    cosine_part = jnp.sqrt(2.0 / beads) * jnp.cos(angle)
    sine_part = jnp.sqrt(2.0 / beads) * jnp.sin(angle)
    edge_part = jnp.sqrt(1.0 / beads) * jnp.cos(jnp.pi * bead_index)
    first = jnp.sqrt(1.0 / beads) * jnp.ones_like(angle)
    table = jnp.where(
        mode_index == 0,
        first,
        jnp.where(
            mode_index < middle, cosine_part, jnp.where(mode_index == middle, edge_part, sine_part)
        ),
    )
    frequency = 2.0 * omega_cycle * jnp.sin(jnp.pi * jnp.arange(beads, dtype=jnp.float32) / beads)
    return (table, frequency)


def pair_force(left_pos, right_pos, left_charge, right_charge):
    separation = left_pos[..., :, None] - right_pos[..., None, :]
    dist_sq = jnp.sum(separation * separation, axis=-3)
    weights = (
        left_charge[..., :, None]
        * right_charge[..., None, :]
        * jnp.exp(-dist_sq / (2.0 * width_sq))
        / width_sq
    )
    return jnp.sum(separation * weights[..., None, :, :], axis=-1)


def propagate(mode_pos, mode_mom, frequency, masses, beads):
    freq_col = frequency[:, None, None]
    mass_row = masses[None, None, :]
    cosine = jnp.cos(freq_col * time_step)
    sine = jnp.sin(freq_col * time_step)
    reach = jnp.where(freq_col > 0, sine / jnp.where(freq_col > 0, freq_col, 1.0), time_step)
    moved_pos = cosine * mode_pos + reach * mode_mom / mass_row
    moved_mom = -mass_row * freq_col * sine * mode_pos + cosine * mode_mom
    spring = (
        jnp.sum(0.5 * mass_row * freq_col * freq_col * moved_pos * moved_pos, axis=(0, 1)) / beads
    )
    return (moved_pos, moved_mom, spring)


def slot_forces(packed):
    slots = packed.shape[0]
    blocks = packed.reshape((slots // 4, 4) + packed.shape[1:])

    def one_block(block_pack):
        return pair_force(
            block_pack[:, 0, :, :3],
            block_pack[:, 1, :, :3],
            block_pack[:, 0, :, 3],
            block_pack[:, 1, :, 3],
        )

    result = lax.map(one_block, blocks)
    return result.reshape((slots,) + result.shape[2:])


def on_device(positions, momenta, charge, masses, pair_local, pair_other, pair_count):
    bead_dev, _, atom_dev = positions.shape
    tile_atoms = 128
    tile_dev = atom_dev // tile_atoms
    atom_count = lax.axis_size("atom")
    bead_count = lax.axis_size("bead")
    beads = bead_dev * bead_count
    tiles = tile_dev * atom_count
    slots = pair_local.shape[0]
    hp = lax.Precision.HIGHEST
    table, frequency = cycle_table(beads)
    sub_atoms = atom_dev // bead_count
    gathered_pos = lax.all_to_all(positions, "bead", split_axis=2, concat_axis=0, tiled=True)
    charge_rows = jnp.broadcast_to(charge[None, None, :], (bead_dev, 1, atom_dev))
    packed = jnp.concatenate([positions, charge_rows], axis=1)
    haloed = extended(packed, (("atom", 2),), atom_dev)
    ext_tiles = jnp.transpose(haloed.reshape(bead_dev, 4, 3 * tile_dev, tile_atoms), (2, 0, 1, 3))
    base_tile = lax.axis_index("atom") * tile_dev - tile_dev
    left_local = (pair_local - base_tile) % tiles
    right_local = (pair_other - base_tile) % tiles
    live_count = pair_count[0]
    slot_ids = jnp.arange(slots)
    live_mask = (slot_ids < live_count).astype(jnp.float32)
    left_block = jnp.take(ext_tiles, left_local, axis=0)
    right_block = jnp.take(ext_tiles, right_local, axis=0)
    left_block = jnp.concatenate(
        [left_block[:, :, :3], left_block[:, :, 3:] * live_mask[:, None, None, None]], axis=2
    )
    forces = slot_forces(jnp.stack([left_block, right_block], axis=1))
    onehot = (left_local[None, :] - tile_dev == jnp.arange(tile_dev)[:, None]).astype(jnp.float32)
    summed = jnp.einsum("ts,sbca->bcta", onehot, forces, precision=hp)
    force = summed.reshape(bead_dev, 3, atom_dev)
    kicked = momenta + 0.5 * time_step * force
    gathered_mom = lax.all_to_all(kicked, "bead", split_axis=2, concat_axis=0, tiled=True)
    mode_pos = jnp.einsum("jk,jca->kca", table, gathered_pos, precision=hp)
    mode_mom = jnp.einsum("jk,jca->kca", table, gathered_mom, precision=hp)
    sub_masses = lax.dynamic_slice_in_dim(masses, lax.axis_index("bead") * sub_atoms, sub_atoms, 0)
    moved_pos, moved_mom, spring_sub = propagate(mode_pos, mode_mom, frequency, sub_masses, beads)
    stacked = jnp.stack([moved_pos, moved_mom], axis=1)
    returned_rows = jnp.einsum("jk,kxca->jxca", table, stacked, precision=hp)
    result = lax.all_to_all(returned_rows, "bead", split_axis=0, concat_axis=3, tiled=True)
    spring = lax.all_gather(spring_sub, "bead", axis=0, tiled=True)
    return (result[:, 0], result[:, 1], spring)


def solution(mesh):
    return jax.shard_map(
        on_device,
        mesh=mesh,
        in_specs=(
            P("bead", None, "atom"),
            P("bead", None, "atom"),
            P("atom"),
            P("atom"),
            P("atom"),
            P("atom"),
            P("atom"),
        ),
        out_specs=(P("bead", None, "atom"), P("bead", None, "atom"), P("atom")),
        check_vma=False,
    )
```

profile of v0, /device:TPU:0, one launch (start us, length us, event | category | flops | bytes accessed | tf_op | source)
XLA Modules:
  0.0 81.9 jit_solution(6459633473460166946)
XLA Ops:
  0.6 0.7 broadcast_in_dim.86
  1.3 0.8 pad_maximum_fusion.3
  2.2 3.0 %collective-permute-start = (f32[4,4,1024]{2,0,1:T(4,128)S(1)}, f32[4,4,1024]{2,0,1:T(4,128)S(1)}, u32[]{:S(2)}, u32[]{:S(2)}) collective-permute-start(f32[4,4,1024]{2,0,1:T(4,128)S(1)} %pad_maximum_fusion.3), channel_id=1, source_target_pairs={{0,1},{1,2},{2,3},{3,0},{4,5},{5,6},{6,7},{7,4},{8,9},{9,10},{10,1... | collective-permute-start | bytes 196616 | tf_op jit(solution)/shard_map/ppermute | solution.py:17
  5.2 1.0 %collective-permute-start.1 = (f32[4,4,1024]{2,0,1:T(4,128)S(1)}, f32[4,4,1024]{2,0,1:T(4,128)S(1)}, u32[]{:S(2)}, u32[]{:S(2)}) collective-permute-start(f32[4,4,1024]{2,0,1:T(4,128)S(1)} %pad_maximum_fusion.3), channel_id=1, source_target_pairs={{1,0},{2,1},{3,2},{0,3},{5,4},{6,5},{7,6},{4,7},{9,8},{10,9},{11,1... | collective-permute-start | bytes 196616 | tf_op jit(solution)/shard_map/ppermute | solution.py:20
  6.2 1.6 %copy.64 = f32[4,3,1024]{0,1,2:T(4,128)S(1)} copy(f32[4,3,1024]{2,0,1:T(4,128)} %param.11) | data formatting | bytes 98304 | tf_op args[0]
  7.8 1.9 %reshape.224 = f32[8,1,1536]{2,1,0:T(1,128)} reshape(f32[1024,3,4]{2,1,0:T(4,128)S(1)} %bitcast.89) | data formatting | bytes 98304
  9.7 5.3 %all-to-all-start = ((f32[8,1,1536]{2,1,0:T(1,128)}), f32[8,1,1536]{2,1,0:T(1,128)S(1)}, u32[]{:S(2)}, u32[]{:S(2)}) async-start(f32[8,1,1536]{2,1,0:T(1,128)} %reshape.224), calls=%async_computation | async-start | bytes 98304 | tf_op jit(solution)/shard_map/all_to_all | solution.py:99
  16.0 0.8 broadcast_multiply_fusion
  17.2 0.7 gather_fusion
  18.3 0.7 gather_fusion.1
  19.4 27.1 %while.10 = (s32[]{:T(128)}, f32[8,4,4,3,128]{4,3,2,1,0:T(4,128)S(1)}, f32[8,4,2,4,4,128]{5,3,1,4,2,0:T(4,128)S(1)}, s32[]{:T(128)}) while((s32[]{:T(128)}, f32[8,4,4,3,128]{4,3,2,1,0:T(4,128)S(1)}, f32[8,4,2,4,4,128]{5,3,1,4,2,0:T(4,128)S(1)}, s32[]{:T(128)}) %tuple.40), condition=%wide.region_3.5_spmd, body=%wide.region_0.4_spmd.sunk | while | flops 5761026 | bytes 4759613 | solution.py:83
  19.5 1.0 %fusion.62 = f32[4,4,128,128]{3,2,1,0:T(8,128)S(1)} fusion(f32[4,4,3,128]{3,2,1,0:T(4,128)S(1)} %copy.92, f32[4,4,3,128]{3,2,1,0:T(4,128)S(1)} %copy.93), kind=kLoop, calls=%fused_computation.4.clone.1 | loop fusion | flops 2097152 | bytes 1097728 | tf_op jit(solution)/shard_map/while/body/eval_jaxpr/reduce_sum | solution.py:47
  20.5 0.3 multiply_multiply_fusion.5
  20.9 1.9 %fusion.63 = f32[4,4,3,128]{3,2,1,0:T(4,128)S(1)} fusion(f32[4,4,128,128]{3,2,1,0:T(8,128)S(1)} %multiply_multiply_fusion.5, f32[4,4,3,128]{3,2,1,0:T(4,128)S(1)} %copy.92, f32[4,4,3,128]{3,2,1,0:T(4,128)S(1)} %copy.93), kind=kLoop, calls=%fused_computation.5.clone.1 | loop fusion | flops 2353152 | bytes 1122304 | tf_op jit(solution)/shard_map/while/body/eval_jaxpr/reduce_sum | solution.py:54
  22.9 1.0 %fusion.62 = f32[4,4,128,128]{3,2,1,0:T(8,128)S(1)} fusion(f32[4,4,3,128]{3,2,1,0:T(4,128)S(1)} %copy.92, f32[4,4,3,128]{3,2,1,0:T(4,128)S(1)} %copy.93), kind=kLoop, calls=%fused_computation.4.clone.1 | loop fusion | flops 2097152 | bytes 1097728 | tf_op jit(solution)/shard_map/while/body/eval_jaxpr/reduce_sum | solution.py:47
  24.3 1.9 %fusion.63 = f32[4,4,3,128]{3,2,1,0:T(4,128)S(1)} fusion(f32[4,4,128,128]{3,2,1,0:T(8,128)S(1)} %multiply_multiply_fusion.5, f32[4,4,3,128]{3,2,1,0:T(4,128)S(1)} %copy.92, f32[4,4,3,128]{3,2,1,0:T(4,128)S(1)} %copy.93), kind=kLoop, calls=%fused_computation.5.clone.1 | loop fusion | flops 2353152 | bytes 1122304 | tf_op jit(solution)/shard_map/while/body/eval_jaxpr/reduce_sum | solution.py:54
  26.3 1.0 %fusion.62 = f32[4,4,128,128]{3,2,1,0:T(8,128)S(1)} fusion(f32[4,4,3,128]{3,2,1,0:T(4,128)S(1)} %copy.92, f32[4,4,3,128]{3,2,1,0:T(4,128)S(1)} %copy.93), kind=kLoop, calls=%fused_computation.4.clone.1 | loop fusion | flops 2097152 | bytes 1097728 | tf_op jit(solution)/shard_map/while/body/eval_jaxpr/reduce_sum | solution.py:47
  27.7 1.9 %fusion.63 = f32[4,4,3,128]{3,2,1,0:T(4,128)S(1)} fusion(f32[4,4,128,128]{3,2,1,0:T(8,128)S(1)} %multiply_multiply_fusion.5, f32[4,4,3,128]{3,2,1,0:T(4,128)S(1)} %copy.92, f32[4,4,3,128]{3,2,1,0:T(4,128)S(1)} %copy.93), kind=kLoop, calls=%fused_computation.5.clone.1 | loop fusion | flops 2353152 | bytes 1122304 | tf_op jit(solution)/shard_map/while/body/eval_jaxpr/reduce_sum | solution.py:54
  29.7 1.0 %fusion.62 = f32[4,4,128,128]{3,2,1,0:T(8,128)S(1)} fusion(f32[4,4,3,128]{3,2,1,0:T(4,128)S(1)} %copy.92, f32[4,4,3,128]{3,2,1,0:T(4,128)S(1)} %copy.93), kind=kLoop, calls=%fused_computation.4.clone.1 | loop fusion | flops 2097152 | bytes 1097728 | tf_op jit(solution)/shard_map/while/body/eval_jaxpr/reduce_sum | solution.py:47
  30.7 0.3 multiply_multiply_fusion.5
  31.1 1.9 %fusion.63 = f32[4,4,3,128]{3,2,1,0:T(4,128)S(1)} fusion(f32[4,4,128,128]{3,2,1,0:T(8,128)S(1)} %multiply_multiply_fusion.5, f32[4,4,3,128]{3,2,1,0:T(4,128)S(1)} %copy.92, f32[4,4,3,128]{3,2,1,0:T(4,128)S(1)} %copy.93), kind=kLoop, calls=%fused_computation.5.clone.1 | loop fusion | flops 2353152 | bytes 1122304 | tf_op jit(solution)/shard_map/while/body/eval_jaxpr/reduce_sum | solution.py:54
  33.0 1.0 %fusion.62 = f32[4,4,128,128]{3,2,1,0:T(8,128)S(1)} fusion(f32[4,4,3,128]{3,2,1,0:T(4,128)S(1)} %copy.92, f32[4,4,3,128]{3,2,1,0:T(4,128)S(1)} %copy.93), kind=kLoop, calls=%fused_computation.4.clone.1 | loop fusion | flops 2097152 | bytes 1097728 | tf_op jit(solution)/shard_map/while/body/eval_jaxpr/reduce_sum | solution.py:47
  34.5 1.9 %fusion.63 = f32[4,4,3,128]{3,2,1,0:T(4,128)S(1)} fusion(f32[4,4,128,128]{3,2,1,0:T(8,128)S(1)} %multiply_multiply_fusion.5, f32[4,4,3,128]{3,2,1,0:T(4,128)S(1)} %copy.92, f32[4,4,3,128]{3,2,1,0:T(4,128)S(1)} %copy.93), kind=kLoop, calls=%fused_computation.5.clone.1 | loop fusion | flops 2353152 | bytes 1122304 | tf_op jit(solution)/shard_map/while/body/eval_jaxpr/reduce_sum | solution.py:54
  36.4 1.0 %fusion.62 = f32[4,4,128,128]{3,2,1,0:T(8,128)S(1)} fusion(f32[4,4,3,128]{3,2,1,0:T(4,128)S(1)} %copy.92, f32[4,4,3,128]{3,2,1,0:T(4,128)S(1)} %copy.93), kind=kLoop, calls=%fused_computation.4.clone.1 | loop fusion | flops 2097152 | bytes 1097728 | tf_op jit(solution)/shard_map/while/body/eval_jaxpr/reduce_sum | solution.py:47
  37.8 1.9 %fusion.63 = f32[4,4,3,128]{3,2,1,0:T(4,128)S(1)} fusion(f32[4,4,128,128]{3,2,1,0:T(8,128)S(1)} %multiply_multiply_fusion.5, f32[4,4,3,128]{3,2,1,0:T(4,128)S(1)} %copy.92, f32[4,4,3,128]{3,2,1,0:T(4,128)S(1)} %copy.93), kind=kLoop, calls=%fused_computation.5.clone.1 | loop fusion | flops 2353152 | bytes 1122304 | tf_op jit(solution)/shard_map/while/body/eval_jaxpr/reduce_sum | solution.py:54
  39.8 1.0 %fusion.62 = f32[4,4,128,128]{3,2,1,0:T(8,128)S(1)} fusion(f32[4,4,3,128]{3,2,1,0:T(4,128)S(1)} %copy.92, f32[4,4,3,128]{3,2,1,0:T(4,128)S(1)} %copy.93), kind=kLoop, calls=%fused_computation.4.clone.1 | loop fusion | flops 2097152 | bytes 1097728 | tf_op jit(solution)/shard_map/while/body/eval_jaxpr/reduce_sum | solution.py:47
  41.2 1.9 %fusion.63 = f32[4,4,3,128]{3,2,1,0:T(4,128)S(1)} fusion(f32[4,4,128,128]{3,2,1,0:T(8,128)S(1)} %multiply_multiply_fusion.5, f32[4,4,3,128]{3,2,1,0:T(4,128)S(1)} %copy.92, f32[4,4,3,128]{3,2,1,0:T(4,128)S(1)} %copy.93), kind=kLoop, calls=%fused_computation.5.clone.1 | loop fusion | flops 2353152 | bytes 1122304 | tf_op jit(solution)/shard_map/while/body/eval_jaxpr/reduce_sum | solution.py:54
  43.2 1.0 %fusion.62 = f32[4,4,128,128]{3,2,1,0:T(8,128)S(1)} fusion(f32[4,4,3,128]{3,2,1,0:T(4,128)S(1)} %copy.92, f32[4,4,3,128]{3,2,1,0:T(4,128)S(1)} %copy.93), kind=kLoop, calls=%fused_computation.4.clone.1 | loop fusion | flops 2097152 | bytes 1097728 | tf_op jit(solution)/shard_map/while/body/eval_jaxpr/reduce_sum | solution.py:47
  44.6 1.9 %fusion.63 = f32[4,4,3,128]{3,2,1,0:T(4,128)S(1)} fusion(f32[4,4,128,128]{3,2,1,0:T(8,128)S(1)} %multiply_multiply_fusion.5, f32[4,4,3,128]{3,2,1,0:T(4,128)S(1)} %copy.92, f32[4,4,3,128]{3,2,1,0:T(4,128)S(1)} %copy.93), kind=kLoop, calls=%fused_computation.5.clone.1 | loop fusion | flops 2353152 | bytes 1122304 | tf_op jit(solution)/shard_map/while/body/eval_jaxpr/reduce_sum | solution.py:54
  46.8 0.9 %copy.73 = f32[4,3,1024]{0,1,2:T(4,128)S(1)} copy(f32[4,3,1024]{2,0,1:T(4,128)S(1)} %add.36) | data formatting | bytes 98304 | tf_op jit(solution)/shard_map/add | solution.py:119
  47.7 1.9 %reshape.222 = f32[8,1,1536]{2,1,0:T(1,128)} reshape(f32[1024,3,4]{2,1,0:T(4,128)S(1)} %bitcast.86) | data formatting | bytes 98304
  49.6 5.1 %all-to-all-start.1 = ((f32[8,1,1536]{2,1,0:T(1,128)}), f32[8,1,1536]{2,1,0:T(1,128)S(1)}, u32[]{:S(2)}, u32[]{:S(2)}) async-start(f32[8,1,1536]{2,1,0:T(1,128)} %reshape.222), calls=%async_computation.1 | async-start | bytes 98304 | tf_op jit(solution)/shard_map/all_to_all | solution.py:120
  54.7 0.5 broadcast.235
  55.2 0.8 reduce.1
  56.0 1.2 %reshape.225 = f32[1024,3,4]{2,1,0:T(4,128)S(1)} reshape(f32[8,1536]{1,0:T(8,128)S(1)} %reduce.1) | data formatting | bytes 98304
  57.2 0.7 copy.65
  57.9 2.6 %all-to-all-done.1 = f32[8,1,1536]{2,1,0:T(1,128)S(1)} async-done(((f32[8,1,1536]{2,1,0:T(1,128)}), f32[8,1,1536]{2,1,0:T(1,128)S(1)}, u32[]{:S(2)}, u32[]{:S(2)}) %all-to-all-start.1) | async-done | bytes 49184 | tf_op jit(solution)/shard_map/all_to_all | solution.py:120
  60.5 0.8 reduce
  61.3 1.2 %reshape.223 = f32[1024,3,4]{2,1,0:T(4,128)S(1)} reshape(f32[8,1536]{1,0:T(8,128)S(1)} %reduce) | data formatting | bytes 98304
  62.5 0.7 copy.74
  63.2 0.4 fusion.10
  63.6 0.4 fusion.8
  64.0 0.4 fusion.4
  64.4 0.7 copy.76
  65.1 3.4 %all-to-all-start.2 = ((f32[32,2,3,128]{3,1,2,0:T(2,128)}), f32[32,2,3,128]{3,1,2,0:T(2,128)S(1)}, u32[]{:S(2)}, u32[]{:S(2)}) async-start(f32[32,2,3,128]{3,1,2,0:T(2,128)} %copy.76), calls=%async_computation.2 | async-start | bytes 196608 | tf_op jit(solution)/shard_map/all_to_all | solution.py:127
  68.5 12.1 %all-gather = f32[8,1,128]{2,1,0:T(1,128)S(1)} all-gather(f32[1,1,128]{2,1,0:T(1,128)S(1)} %multiply_bitcast_fusion), channel_id=1, replica_groups=mesh['bead'=8,'atom'=4] {'bead'}, dimensions={0}, use_global_device_ids=true | all-gather | bytes 4608 | tf_op jit(solution)/shard_map/all_gather | solution.py:128
  80.7 0.6 slice_bitcast_fusion.4
  81.3 0.6 copy.104
  (98 shorter events, 4.4 us)
Async XLA Ops:
  2.1 12.8 %copy-start.2 = (s32[32]{0:T(128)S(1)}, s32[32]{0:T(128)}, u32[]{:S(2)}) copy-start(s32[32]{0:T(128)} %param.15) | copy-start | bytes 388
  2.1 13.8 %copy-start.3 = (s32[32]{0:T(128)S(1)}, s32[32]{0:T(128)}, u32[]{:S(2)}) copy-start(s32[32]{0:T(128)} %param.16) | copy-start | bytes 388
  2.2 14.7 %copy-start = (f32[4,3,1024]{2,0,1:T(4,128)S(1)}, f32[4,3,1024]{2,0,1:T(4,128)}, u32[]{:S(2)}) copy-start(f32[4,3,1024]{2,0,1:T(4,128)} %param.11) | copy-start | bytes 147460
  2.2 14.7 %collective-permute-start = (f32[4,4,1024]{2,0,1:T(4,128)S(1)}, f32[4,4,1024]{2,0,1:T(4,128)S(1)}, u32[]{:S(2)}, u32[]{:S(2)}) collective-permute-start(f32[4,4,1024]{2,0,1:T(4,128)S(1)} %pad_maximum_fusion.3), channel_id=1, source_target_pairs={{0,1},{1,2},{2,3},{3,0},{4,5},{5,6},{6,7},{7,4},{8,9},{9,10},{10,1... | collective-permute-start | bytes 196616 | tf_op jit(solution)/shard_map/ppermute | solution.py:17
  5.2 11.7 %collective-permute-start.1 = (f32[4,4,1024]{2,0,1:T(4,128)S(1)}, f32[4,4,1024]{2,0,1:T(4,128)S(1)}, u32[]{:S(2)}, u32[]{:S(2)}) collective-permute-start(f32[4,4,1024]{2,0,1:T(4,128)S(1)} %pad_maximum_fusion.3), channel_id=1, source_target_pairs={{1,0},{2,1},{3,2},{0,3},{5,4},{6,5},{7,6},{4,7},{9,8},{10,9},{11,1... | collective-permute-start | bytes 196616 | tf_op jit(solution)/shard_map/ppermute | solution.py:20
  9.7 39.9 %all-to-all-start = ((f32[8,1,1536]{2,1,0:T(1,128)}), f32[8,1,1536]{2,1,0:T(1,128)S(1)}, u32[]{:S(2)}, u32[]{:S(2)}) async-start(f32[8,1,1536]{2,1,0:T(1,128)} %reshape.224), calls=%async_computation | async-start | bytes 98304 | tf_op jit(solution)/shard_map/all_to_all | solution.py:99
  19.4 27.4 %copy-start.1 = (f32[4,3,1024]{2,0,1:T(4,128)S(1)}, f32[4,3,1024]{2,0,1:T(4,128)}, u32[]{:S(2)}) copy-start(f32[4,3,1024]{2,0,1:T(4,128)} %param.12) | copy-start | bytes 147460
  49.6 10.9 %all-to-all-start.1 = ((f32[8,1,1536]{2,1,0:T(1,128)}), f32[8,1,1536]{2,1,0:T(1,128)S(1)}, u32[]{:S(2)}, u32[]{:S(2)}) async-start(f32[8,1,1536]{2,1,0:T(1,128)} %reshape.222), calls=%async_computation.1 | async-start | bytes 98304 | tf_op jit(solution)/shard_map/all_to_all | solution.py:120
  65.1 15.5 %all-to-all-start.2 = ((f32[32,2,3,128]{3,1,2,0:T(2,128)}), f32[32,2,3,128]{3,1,2,0:T(2,128)S(1)}, u32[]{:S(2)}, u32[]{:S(2)}) async-start(f32[32,2,3,128]{3,1,2,0:T(2,128)} %copy.76), calls=%async_computation.2 | async-start | bytes 196608 | tf_op jit(solution)/shard_map/all_to_all | solution.py:127
where the time goes:
time: 82.5 us; the launch traced here: 81.9 us
  other arithmetic  30.1 us (36%)
  starting transfers between devices  17.8 us (22%)
  local copies, waits for them, and re-layouts  15.6 us (19%)
  blocking collectives  12.1 us (15%)
  waiting for transfers between devices  2.63 us (3%)
  between operations  1.65 us (2%)
  matrix products  1.39 us (2%)
    reduce_sum x8, other arithmetic, pair_force(): return jnp.sum(separation * weights[..., None, :, :], axis=-1)  14.9 us
    all_gather x1, blocking collectives, on_device(): spring = lax.all_gather(spring_sub, 'bead', axis=0, tiled=True)  12.1 us
    unnamed x14, local copies, waits for them, and re-layouts  8.41 us
    reduce_sum x8, other arithmetic, pair_force(): dist_sq = jnp.sum(separation * separation, axis=-3)  8.35 us
    all_to_all x1, starting transfers between devices, on_device(): lax.all_to_all(positions, 'bead', split_axis=2, concat_axis=0, tiled=True)  5.29 us
    all_to_all x1, starting transfers between devices, on_device(): lax.all_to_all(kicked, 'bead', split_axis=2, concat_axis=0, tiled=True)  5.09 us
    all_to_all x1, starting transfers between devices, on_device(): lax.all_to_all(returned_rows, 'bead', split_axis=0, concat_axis=3, tiled=...  3.36 us
    ppermute x1, starting transfers between devices, extended(): lax.ppermute(lax.slice_in_dim(block, block.shape[dim] - width, None, axis...  3.02 us
  transfers between devices with their start and end apart: 5, of which 1 were waited for; matrix products, arithmetic and copies ran while one was open for 49% of the time, Pallas kernels for 0%

commit v1 on v0

--- a/solution.py
+++ b/solution.py
@@ -96,7 +96,12 @@
     hp = lax.Precision.HIGHEST
     table, frequency = cycle_table(beads)
     sub_atoms = atom_dev // bead_count
-    gathered_pos = lax.all_to_all(positions, "bead", split_axis=2, concat_axis=0, tiled=True)
+    gathered_pos = jnp.concatenate(
+        lax.all_to_all(
+            jnp.stack(jnp.split(positions, lax.axis_size("bead"), axis=2)), "bead", 0, 0
+        ),
+        axis=0,
+    )
     charge_rows = jnp.broadcast_to(charge[None, None, :], (bead_dev, 1, atom_dev))
     packed = jnp.concatenate([positions, charge_rows], axis=1)
     haloed = extended(packed, (("atom", 2),), atom_dev)

time: 82.5 us -> 92.1 us (1.12)
  local copies, waits for them, and re-layouts: 15.6 us -> 20.5 us
  waiting for transfers between devices: 2.63 us -> 5.81 us
  other arithmetic: 30.1 us -> 31.5 us
    unnamed x14 -> x12, local copies, waits for them, and re-layouts: 8.41 us -> 12.7 us
    all_to_all x1, waiting for transfers between devices: 2.61 us -> 5.8 us  [on_device(): lax.all_to_all(kicked, 'bead', split_axis=2, concat_axis=0, tiled=True)]
    another operation x0 -> x1, local copies, waits for them, and re-layouts: none -> 1.28 us  [on_device(): jnp.stack(jnp.split(positions, lax.axis_size('bead'), axis=2))]
  transfers between devices with their start and end apart: 5 -> 5, of which waited for: 1 -> 1; matrix products, arithmetic and copies ran while one was open for 49% -> 50% of each run, Pallas kernels for 0% -> 0%
where the time goes in v1:
time: 92.1 us; the launch traced here: 91.2 us
  other arithmetic  31.5 us (34%)
  local copies, waits for them, and re-layouts  20.5 us (22%)
  starting transfers between devices  17.8 us (19%)
  blocking collectives  12.1 us (13%)
  waiting for transfers between devices  5.81 us (6%)
  between operations  1.56 us (2%)
  matrix products  1.39 us (2%)
    reduce_sum x8, other arithmetic, pair_force(): return jnp.sum(separation * weights[..., None, :, :], axis=-1)  14.9 us
    unnamed x12, local copies, waits for them, and re-layouts  12.7 us
    all_gather x1, blocking collectives, on_device(): spring = lax.all_gather(spring_sub, 'bead', axis=0, tiled=True)  12.1 us
    reduce_sum x8, other arithmetic, pair_force(): dist_sq = jnp.sum(separation * separation, axis=-3)  8.35 us
    all_to_all x1, waiting for transfers between devices, on_device(): lax.all_to_all(kicked, 'bead', split_axis=2, concat_axis=0, tiled=True)  5.8 us
    all_to_all x1, starting transfers between devices, on_device(): lax.all_to_all(jnp.stack(jnp.split(positions, lax.axis_size('bead'), axis...  5.29 us
    all_to_all x1, starting transfers between devices, on_device(): lax.all_to_all(kicked, 'bead', split_axis=2, concat_axis=0, tiled=True)  5.1 us
    all_to_all x1, starting transfers between devices, on_device(): lax.all_to_all(returned_rows, 'bead', split_axis=0, concat_axis=3, tiled=...  3.36 us
  transfers between devices with their start and end apart: 5, of which 1 were waited for; matrix products, arithmetic and copies ran while one was open for 50% of the time, Pallas kernels for 0%

profile of v1, /device:TPU:0, one launch (start us, length us, event | category | flops | bytes accessed | tf_op | source)
XLA Modules:
  0.0 91.2 jit_solution(3047961756806299245)
XLA Ops:
  0.6 0.7 broadcast_in_dim.86
  1.3 0.8 pad_maximum_fusion.3
  2.1 3.0 %collective-permute-start = (f32[4,4,1024]{2,0,1:T(4,128)S(1)}, f32[4,4,1024]{2,0,1:T(4,128)S(1)}, u32[]{:S(2)}, u32[]{:S(2)}) collective-permute-start(f32[4,4,1024]{2,0,1:T(4,128)S(1)} %pad_maximum_fusion.3), channel_id=1, source_target_pairs={{0,1},{1,2},{2,3},{3,0},{4,5},{5,6},{6,7},{7,4},{8,9},{9,10},{10,1... | collective-permute-start | bytes 196616 | tf_op jit(solution)/shard_map/ppermute | solution.py:17
  5.2 1.0 %collective-permute-start.1 = (f32[4,4,1024]{2,0,1:T(4,128)S(1)}, f32[4,4,1024]{2,0,1:T(4,128)S(1)}, u32[]{:S(2)}, u32[]{:S(2)}) collective-permute-start(f32[4,4,1024]{2,0,1:T(4,128)S(1)} %pad_maximum_fusion.3), channel_id=1, source_target_pairs={{1,0},{2,1},{3,2},{0,3},{5,4},{6,5},{7,6},{4,7},{9,8},{10,9},{11,1... | collective-permute-start | bytes 196616 | tf_op jit(solution)/shard_map/ppermute | solution.py:20
  6.2 1.3 %constant_dynamic-update-slice_fusion.7 = f32[8,4,3,128]{3,1,2,0:T(4,128)} fusion(f32[4,3,1024]{2,0,1:T(4,128)} %param.11), kind=kLoop, calls=%fused_computation.41 | loop fusion | bytes 12288
  7.5 1.3 %constant_dynamic-update-slice_fusion.6 = f32[8,4,3,128]{3,1,2,0:T(4,128)} fusion(f32[8,4,3,128]{3,1,2,0:T(4,128)} %constant_dynamic-update-slice_fusion.7, f32[4,3,1024]{2,0,1:T(4,128)} %param.11), kind=kLoop, calls=%fused_computation.40 | loop fusion | bytes 12288
  8.7 1.3 %constant_dynamic-update-slice_fusion.5 = f32[8,4,3,128]{3,1,2,0:T(4,128)} fusion(f32[8,4,3,128]{3,1,2,0:T(4,128)} %constant_dynamic-update-slice_fusion.6, f32[4,3,1024]{2,0,1:T(4,128)} %param.11), kind=kLoop, calls=%fused_computation.39 | loop fusion | bytes 12288
  10.0 1.3 %constant_dynamic-update-slice_fusion.4 = f32[8,4,3,128]{3,1,2,0:T(4,128)} fusion(f32[8,4,3,128]{3,1,2,0:T(4,128)} %constant_dynamic-update-slice_fusion.5, f32[4,3,1024]{2,0,1:T(4,128)} %param.11), kind=kLoop, calls=%fused_computation.38 | loop fusion | bytes 12288
  11.3 1.3 %constant_dynamic-update-slice_fusion.3 = f32[8,4,3,128]{3,1,2,0:T(4,128)} fusion(f32[8,4,3,128]{3,1,2,0:T(4,128)} %constant_dynamic-update-slice_fusion.4, f32[4,3,1024]{2,0,1:T(4,128)} %param.11), kind=kLoop, calls=%fused_computation.37 | loop fusion | bytes 12288
  12.6 1.3 %constant_dynamic-update-slice_fusion.2 = f32[8,4,3,128]{3,1,2,0:T(4,128)} fusion(f32[8,4,3,128]{3,1,2,0:T(4,128)} %constant_dynamic-update-slice_fusion.3, f32[4,3,1024]{2,0,1:T(4,128)} %param.11), kind=kLoop, calls=%fused_computation.36 | loop fusion | bytes 12288
  13.9 1.3 %constant_dynamic-update-slice_fusion.1 = f32[8,4,3,128]{3,1,2,0:T(4,128)} fusion(f32[8,4,3,128]{3,1,2,0:T(4,128)} %constant_dynamic-update-slice_fusion.2, f32[4,3,1024]{2,0,1:T(4,128)} %param.11), kind=kLoop, calls=%fused_computation.35 | loop fusion | bytes 12288
  15.2 1.3 %constant_dynamic-update-slice_fusion = f32[8,4,3,128]{3,1,2,0:T(4,128)} fusion(f32[8,4,3,128]{3,1,2,0:T(4,128)} %constant_dynamic-update-slice_fusion.1, f32[4,3,1024]{2,0,1:T(4,128)} %param.11), kind=kLoop, calls=%fused_computation.34 | loop fusion | bytes 12288 | tf_op jit(solution)/shard_map/stack | solution.py:101
  16.5 5.3 %all-to-all-start = ((f32[8,4,3,128]{3,1,2,0:T(4,128)}), f32[8,4,3,128]{3,1,2,0:T(4,128)S(1)}, u32[]{:S(2)}, u32[]{:S(2)}) async-start(f32[8,4,3,128]{3,1,2,0:T(4,128)} %constant_dynamic-update-slice_fusion), calls=%async_computation | async-start | bytes 98304 | tf_op jit(solution)/shard_map/all_to_all | solution.py:100
  21.8 0.7 broadcast_add_fusion
  22.7 0.7 compare_and_fusion
  24.0 0.8 broadcast_multiply_fusion
  24.9 0.8 pad_maximum_fusion.2
  26.0 0.7 gather_fusion
  27.2 0.7 gather_fusion.1
  28.2 27.1 %while.10 = (s32[]{:T(128)}, f32[8,4,4,3,128]{4,3,2,1,0:T(4,128)S(1)}, f32[8,4,2,4,4,128]{5,3,1,4,2,0:T(4,128)S(1)}, s32[]{:T(128)}) while((s32[]{:T(128)}, f32[8,4,4,3,128]{4,3,2,1,0:T(4,128)S(1)}, f32[8,4,2,4,4,128]{5,3,1,4,2,0:T(4,128)S(1)}, s32[]{:T(128)}) %tuple.41), condition=%wide.region_3.5_spmd, body=%wide.region_0.4_spmd.sunk | while | flops 5761026 | bytes 4759613 | solution.py:83
  28.3 1.0 %fusion.62 = f32[4,4,128,128]{3,2,1,0:T(8,128)S(1)} fusion(f32[4,4,3,128]{3,2,1,0:T(4,128)S(1)} %copy.89, f32[4,4,3,128]{3,2,1,0:T(4,128)S(1)} %copy.90), kind=kLoop, calls=%fused_computation.4.clone.1 | loop fusion | flops 2097152 | bytes 1097728 | tf_op jit(solution)/shard_map/while/body/eval_jaxpr/reduce_sum | solution.py:47
  29.7 1.9 %fusion.63 = f32[4,4,3,128]{3,2,1,0:T(4,128)S(1)} fusion(f32[4,4,128,128]{3,2,1,0:T(8,128)S(1)} %multiply_multiply_fusion.5, f32[4,4,3,128]{3,2,1,0:T(4,128)S(1)} %copy.89, f32[4,4,3,128]{3,2,1,0:T(4,128)S(1)} %copy.90), kind=kLoop, calls=%fused_computation.5.clone.1 | loop fusion | flops 2353152 | bytes 1122304 | tf_op jit(solution)/shard_map/while/body/eval_jaxpr/reduce_sum | solution.py:54
  31.7 1.0 %fusion.62 = f32[4,4,128,128]{3,2,1,0:T(8,128)S(1)} fusion(f32[4,4,3,128]{3,2,1,0:T(4,128)S(1)} %copy.89, f32[4,4,3,128]{3,2,1,0:T(4,128)S(1)} %copy.90), kind=kLoop, calls=%fused_computation.4.clone.1 | loop fusion | flops 2097152 | bytes 1097728 | tf_op jit(solution)/shard_map/while/body/eval_jaxpr/reduce_sum | solution.py:47
  33.1 1.9 %fusion.63 = f32[4,4,3,128]{3,2,1,0:T(4,128)S(1)} fusion(f32[4,4,128,128]{3,2,1,0:T(8,128)S(1)} %multiply_multiply_fusion.5, f32[4,4,3,128]{3,2,1,0:T(4,128)S(1)} %copy.89, f32[4,4,3,128]{3,2,1,0:T(4,128)S(1)} %copy.90), kind=kLoop, calls=%fused_computation.5.clone.1 | loop fusion | flops 2353152 | bytes 1122304 | tf_op jit(solution)/shard_map/while/body/eval_jaxpr/reduce_sum | solution.py:54
  35.1 1.0 %fusion.62 = f32[4,4,128,128]{3,2,1,0:T(8,128)S(1)} fusion(f32[4,4,3,128]{3,2,1,0:T(4,128)S(1)} %copy.89, f32[4,4,3,128]{3,2,1,0:T(4,128)S(1)} %copy.90), kind=kLoop, calls=%fused_computation.4.clone.1 | loop fusion | flops 2097152 | bytes 1097728 | tf_op jit(solution)/shard_map/while/body/eval_jaxpr/reduce_sum | solution.py:47
  36.5 1.9 %fusion.63 = f32[4,4,3,128]{3,2,1,0:T(4,128)S(1)} fusion(f32[4,4,128,128]{3,2,1,0:T(8,128)S(1)} %multiply_multiply_fusion.5, f32[4,4,3,128]{3,2,1,0:T(4,128)S(1)} %copy.89, f32[4,4,3,128]{3,2,1,0:T(4,128)S(1)} %copy.90), kind=kLoop, calls=%fused_computation.5.clone.1 | loop fusion | flops 2353152 | bytes 1122304 | tf_op jit(solution)/shard_map/while/body/eval_jaxpr/reduce_sum | solution.py:54
  38.5 1.0 %fusion.62 = f32[4,4,128,128]{3,2,1,0:T(8,128)S(1)} fusion(f32[4,4,3,128]{3,2,1,0:T(4,128)S(1)} %copy.89, f32[4,4,3,128]{3,2,1,0:T(4,128)S(1)} %copy.90), kind=kLoop, calls=%fused_computation.4.clone.1 | loop fusion | flops 2097152 | bytes 1097728 | tf_op jit(solution)/shard_map/while/body/eval_jaxpr/reduce_sum | solution.py:47
  39.9 1.9 %fusion.63 = f32[4,4,3,128]{3,2,1,0:T(4,128)S(1)} fusion(f32[4,4,128,128]{3,2,1,0:T(8,128)S(1)} %multiply_multiply_fusion.5, f32[4,4,3,128]{3,2,1,0:T(4,128)S(1)} %copy.89, f32[4,4,3,128]{3,2,1,0:T(4,128)S(1)} %copy.90), kind=kLoop, calls=%fused_computation.5.clone.1 | loop fusion | flops 2353152 | bytes 1122304 | tf_op jit(solution)/shard_map/while/body/eval_jaxpr/reduce_sum | solution.py:54
  41.9 1.0 %fusion.62 = f32[4,4,128,128]{3,2,1,0:T(8,128)S(1)} fusion(f32[4,4,3,128]{3,2,1,0:T(4,128)S(1)} %copy.89, f32[4,4,3,128]{3,2,1,0:T(4,128)S(1)} %copy.90), kind=kLoop, calls=%fused_computation.4.clone.1 | loop fusion | flops 2097152 | bytes 1097728 | tf_op jit(solution)/shard_map/while/body/eval_jaxpr/reduce_sum | solution.py:47
  43.3 1.9 %fusion.63 = f32[4,4,3,128]{3,2,1,0:T(4,128)S(1)} fusion(f32[4,4,128,128]{3,2,1,0:T(8,128)S(1)} %multiply_multiply_fusion.5, f32[4,4,3,128]{3,2,1,0:T(4,128)S(1)} %copy.89, f32[4,4,3,128]{3,2,1,0:T(4,128)S(1)} %copy.90), kind=kLoop, calls=%fused_computation.5.clone.1 | loop fusion | flops 2353152 | bytes 1122304 | tf_op jit(solution)/shard_map/while/body/eval_jaxpr/reduce_sum | solution.py:54
  45.3 1.0 %fusion.62 = f32[4,4,128,128]{3,2,1,0:T(8,128)S(1)} fusion(f32[4,4,3,128]{3,2,1,0:T(4,128)S(1)} %copy.89, f32[4,4,3,128]{3,2,1,0:T(4,128)S(1)} %copy.90), kind=kLoop, calls=%fused_computation.4.clone.1 | loop fusion | flops 2097152 | bytes 1097728 | tf_op jit(solution)/shard_map/while/body/eval_jaxpr/reduce_sum | solution.py:47
  46.7 1.9 %fusion.63 = f32[4,4,3,128]{3,2,1,0:T(4,128)S(1)} fusion(f32[4,4,128,128]{3,2,1,0:T(8,128)S(1)} %multiply_multiply_fusion.5, f32[4,4,3,128]{3,2,1,0:T(4,128)S(1)} %copy.89, f32[4,4,3,128]{3,2,1,0:T(4,128)S(1)} %copy.90), kind=kLoop, calls=%fused_computation.5.clone.1 | loop fusion | flops 2353152 | bytes 1122304 | tf_op jit(solution)/shard_map/while/body/eval_jaxpr/reduce_sum | solution.py:54
  48.7 1.0 %fusion.62 = f32[4,4,128,128]{3,2,1,0:T(8,128)S(1)} fusion(f32[4,4,3,128]{3,2,1,0:T(4,128)S(1)} %copy.89, f32[4,4,3,128]{3,2,1,0:T(4,128)S(1)} %copy.90), kind=kLoop, calls=%fused_computation.4.clone.1 | loop fusion | flops 2097152 | bytes 1097728 | tf_op jit(solution)/shard_map/while/body/eval_jaxpr/reduce_sum | solution.py:47
  50.1 1.9 %fusion.63 = f32[4,4,3,128]{3,2,1,0:T(4,128)S(1)} fusion(f32[4,4,128,128]{3,2,1,0:T(8,128)S(1)} %multiply_multiply_fusion.5, f32[4,4,3,128]{3,2,1,0:T(4,128)S(1)} %copy.89, f32[4,4,3,128]{3,2,1,0:T(4,128)S(1)} %copy.90), kind=kLoop, calls=%fused_computation.5.clone.1 | loop fusion | flops 2353152 | bytes 1122304 | tf_op jit(solution)/shard_map/while/body/eval_jaxpr/reduce_sum | solution.py:54
  52.0 1.0 %fusion.62 = f32[4,4,128,128]{3,2,1,0:T(8,128)S(1)} fusion(f32[4,4,3,128]{3,2,1,0:T(4,128)S(1)} %copy.89, f32[4,4,3,128]{3,2,1,0:T(4,128)S(1)} %copy.90), kind=kLoop, calls=%fused_computation.4.clone.1 | loop fusion | flops 2097152 | bytes 1097728 | tf_op jit(solution)/shard_map/while/body/eval_jaxpr/reduce_sum | solution.py:47
  53.5 1.9 %fusion.63 = f32[4,4,3,128]{3,2,1,0:T(4,128)S(1)} fusion(f32[4,4,128,128]{3,2,1,0:T(8,128)S(1)} %multiply_multiply_fusion.5, f32[4,4,3,128]{3,2,1,0:T(4,128)S(1)} %copy.89, f32[4,4,3,128]{3,2,1,0:T(4,128)S(1)} %copy.90), kind=kLoop, calls=%fused_computation.5.clone.1 | loop fusion | flops 2353152 | bytes 1122304 | tf_op jit(solution)/shard_map/while/body/eval_jaxpr/reduce_sum | solution.py:54
  55.7 0.9 copy.70
  56.5 1.9 %reshape.226 = f32[8,1,1536]{2,1,0:T(1,128)} reshape(f32[1024,3,4]{2,1,0:T(4,128)S(1)} %bitcast.97) | data formatting | bytes 98304
  58.4 5.1 %all-to-all-start.1 = ((f32[8,1,1536]{2,1,0:T(1,128)}), f32[8,1,1536]{2,1,0:T(1,128)S(1)}, u32[]{:S(2)}, u32[]{:S(2)}) async-start(f32[8,1,1536]{2,1,0:T(1,128)} %reshape.226), calls=%async_computation.1 | async-start | bytes 98304 | tf_op jit(solution)/shard_map/all_to_all | solution.py:125
  63.5 5.8 %all-to-all-done.1 = f32[8,1,1536]{2,1,0:T(1,128)S(1)} async-done(((f32[8,1,1536]{2,1,0:T(1,128)}), f32[8,1,1536]{2,1,0:T(1,128)S(1)}, u32[]{:S(2)}, u32[]{:S(2)}) %all-to-all-start.1) | async-done | bytes 49184 | tf_op jit(solution)/shard_map/all_to_all | solution.py:125
  69.9 0.8 reduce
  70.6 1.2 %reshape.227 = f32[1024,3,4]{2,1,0:T(4,128)S(1)} reshape(f32[8,1536]{1,0:T(8,128)S(1)} %reduce) | data formatting | bytes 98304
  71.9 0.7 copy.71
  73.7 0.7 copy.73
  74.4 3.4 %all-to-all-start.2 = ((f32[32,2,3,128]{3,1,2,0:T(2,128)}), f32[32,2,3,128]{3,1,2,0:T(2,128)S(1)}, u32[]{:S(2)}, u32[]{:S(2)}) async-start(f32[32,2,3,128]{3,1,2,0:T(2,128)} %copy.73), calls=%async_computation.2 | async-start | bytes 196608 | tf_op jit(solution)/shard_map/all_to_all | solution.py:132
  77.8 12.1 %all-gather = f32[8,1,128]{2,1,0:T(1,128)S(1)} all-gather(f32[1,1,128]{2,1,0:T(1,128)S(1)} %multiply_bitcast_fusion), channel_id=1, replica_groups=mesh['bead'=8,'atom'=4] {'bead'}, dimensions={0}, use_global_device_ids=true | all-gather | bytes 4608 | tf_op jit(solution)/shard_map/all_gather | solution.py:133
  90.0 0.6 slice_bitcast_fusion.4
  90.7 0.6 copy.108
  (95 shorter events, 6.6 us)
Async XLA Ops:
  2.1 22.8 %collective-permute-start = (f32[4,4,1024]{2,0,1:T(4,128)S(1)}, f32[4,4,1024]{2,0,1:T(4,128)S(1)}, u32[]{:S(2)}, u32[]{:S(2)}) collective-permute-start(f32[4,4,1024]{2,0,1:T(4,128)S(1)} %pad_maximum_fusion.3), channel_id=1, source_target_pairs={{0,1},{1,2},{2,3},{3,0},{4,5},{5,6},{6,7},{7,4},{8,9},{9,10},{10,1... | collective-permute-start | bytes 196616 | tf_op jit(solution)/shard_map/ppermute | solution.py:17
  5.2 19.7 %collective-permute-start.1 = (f32[4,4,1024]{2,0,1:T(4,128)S(1)}, f32[4,4,1024]{2,0,1:T(4,128)S(1)}, u32[]{:S(2)}, u32[]{:S(2)}) collective-permute-start(f32[4,4,1024]{2,0,1:T(4,128)S(1)} %pad_maximum_fusion.3), channel_id=1, source_target_pairs={{1,0},{2,1},{3,2},{0,3},{5,4},{6,5},{7,6},{4,7},{9,8},{10,9},{11,1... | collective-permute-start | bytes 196616 | tf_op jit(solution)/shard_map/ppermute | solution.py:20
  16.5 42.0 %all-to-all-start = ((f32[8,4,3,128]{3,1,2,0:T(4,128)}), f32[8,4,3,128]{3,1,2,0:T(4,128)S(1)}, u32[]{:S(2)}, u32[]{:S(2)}) async-start(f32[8,4,3,128]{3,1,2,0:T(4,128)} %constant_dynamic-update-slice_fusion), calls=%async_computation | async-start | bytes 98304 | tf_op jit(solution)/shard_map/all_to_all | solution.py:100
  28.2 27.4 %copy-start = (f32[4,3,1024]{2,0,1:T(4,128)S(1)}, f32[4,3,1024]{2,0,1:T(4,128)}, u32[]{:S(2)}) copy-start(f32[4,3,1024]{2,0,1:T(4,128)} %param.12) | copy-start | bytes 147460
  58.4 10.9 %all-to-all-start.1 = ((f32[8,1,1536]{2,1,0:T(1,128)}), f32[8,1,1536]{2,1,0:T(1,128)S(1)}, u32[]{:S(2)}, u32[]{:S(2)}) async-start(f32[8,1,1536]{2,1,0:T(1,128)} %reshape.226), calls=%async_computation.1 | async-start | bytes 98304 | tf_op jit(solution)/shard_map/all_to_all | solution.py:125
  74.4 15.5 %all-to-all-start.2 = ((f32[32,2,3,128]{3,1,2,0:T(2,128)}), f32[32,2,3,128]{3,1,2,0:T(2,128)S(1)}, u32[]{:S(2)}, u32[]{:S(2)}) async-start(f32[32,2,3,128]{3,1,2,0:T(2,128)} %copy.73), calls=%async_computation.2 | async-start | bytes 196608 | tf_op jit(solution)/shard_map/all_to_all | solution.py:132
